TPU v7x, 32 devices: a whole 2x2x4 slice. The times are simulated.
32 devices in a mesh: groups: 1, role: 2 (over core), dev: 16 (over z, y, x).
Axes of the slice: x: 2, y: 2, z: 4, core: 2. Of those that a mesh axis runs over, the one named last changes fastest.
Arguments:
- prompt_hidden: bfloat16 [4096, 4096], P(('groups', 'dev')), may hold values from -6 to 6
- norm_gain: float32 [4096], replicated, may hold values from 0.25 to 1.75
- kv_weight: bfloat16 [4096, 4, 2, 128], P(None, 'role'), may hold values from -0.09375 to 0.09375
- prompt_excess: int32 [4], P('groups'), may hold values from 1 to 1536, 2048 in all
- prompt_owner: int32 [4], P('groups'), may hold values from 0 to 15, as said below
- response_counts: int32 [4], P('groups'), may hold values from 1 to 5, as said below
- queries: bfloat16 [256, 16, 128], P(('groups', 'dev'), 'role'), may hold values from -256 to 256
- new_kv: bfloat16 [256, 4, 2, 128], P(('groups', 'dev'), 'role'), may hold values from -6 to 6
- response_cache: bfloat16 [256, 256, 4, 2, 128], P(('groups', 'dev'), None, 'role'), may hold values from -6 to 6
- positions: int32 [256], P(('groups', 'dev')), may hold values from 0 to 256
- out_weight: bfloat16 [16, 128, 4096], P('role', None, 'dev'), may hold values from -0.125 to 0.125
Outputs:
- attended: bfloat16 [256, 16, 128], P(('groups', 'dev'), 'role')
- block_out: bfloat16 [256, 4096], P(('groups', 'role'), 'dev')
Inputs may be any that keep to these rules, and one draw needn't show every extreme that they name: `prompt_owner`: no device along dev owns more than two prompts, and some device owns exactly two. `response_counts`: some prompt has exactly 5 responses.
All inputs are finite; a program needn't handle non-finite values.
Results may differ from a plain program's by a relative error of at most 0.0065.
Values may be sent and summed in bfloat16 or wider, within the bound.
A program may use at most 192 MiB of HBM per device.

v0:
```python
import jax
import jax.numpy as jnp
from jax import lax
from jax.sharding import PartitionSpec as P

RESP = 5
PROMPT_MIN = 512


rope_base = 500000.0


def merged_2(part, axis, combine):
    gathered = jax.tree.map(lambda a: lax.all_gather(a, axis), part)

    def take(source):
        return jax.tree.map(lambda a: lax.dynamic_index_in_dim(a, source, 0, False), gathered)

    return lax.fori_loop(
        1, lax.axis_size(axis), lambda source, state: combine(state, take(source)), take(0)
    )


def rotate(vectors, offsets):
    half = vectors.shape[-1] // 2
    freq = rope_base ** (-jnp.arange(half, dtype=jnp.float32) * 2.0 / vectors.shape[-1])
    angles = offsets.astype(jnp.float32)[:, None] * freq[None, :]
    cosine = jnp.cos(angles)[:, None, :]
    sine = jnp.sin(angles)[:, None, :]
    first = vectors[..., :half]
    second = vectors[..., half:]
    return jnp.concatenate(
        [first * cosine - second * sine, second * cosine + first * sine], axis=-1
    )


def prompt_layout(prompt_excess, token_index):
    lengths = PROMPT_MIN + prompt_excess
    ends = jnp.cumsum(lengths)
    starts = ends - lengths
    prompt_id = jnp.sum((token_index[:, None] >= ends[None, :]).astype(jnp.int32), axis=1)
    member = prompt_id[:, None] == jnp.arange(lengths.shape[0], dtype=jnp.int32)[None, :]
    offsets = token_index - jnp.sum(jnp.where(member, starts[None, :], 0), axis=1)
    return (member, offsets, starts, lengths)


def first_slots(owner, counts):
    order = jnp.arange(owner.shape[0], dtype=jnp.int32)
    earlier = (owner[:, None] == owner[None, :]) & (order[None, :] < order[:, None])
    return jnp.sum(jnp.where(earlier, counts[None, :], 0), axis=1)


def slot_prompts(owner, counts, slot_device, slot_index):
    order = jnp.arange(owner.shape[0], dtype=jnp.int32)
    first = first_slots(owner, counts)
    match = (
        (owner[None, :] == slot_device[:, None])
        & (first[None, :] <= slot_index[:, None])
        & (slot_index[:, None] < first[None, :] + counts[None, :])
    )
    present = jnp.any(match, axis=1)
    chosen = jnp.sum(jnp.where(match, order[None, :], 0), axis=1)
    return (chosen, present)


def softmax_state(scores, valid):
    scores = jnp.where(valid[:, None, None, :], scores, -1e30)
    peak = jnp.max(scores, axis=-1)
    weights = jnp.where(valid[:, None, None, :], jnp.exp(scores - peak[..., None]), 0.0)
    return (peak, jnp.sum(weights, axis=-1), weights.astype(jnp.bfloat16))


def state_each(query, keys, values, valid, scale):
    scores = jnp.einsum("sngd,slnd->sngl", query, keys, preferred_element_type=jnp.float32) * scale
    peak, total, rounded = softmax_state(scores, valid)
    mixed = jnp.einsum("sngl,slnd->sngd", rounded, values, preferred_element_type=jnp.float32)
    return (peak, total, mixed)


def state_shared(query, keys, values, valid, scale):
    scores = jnp.einsum("sngd,lnd->sngl", query, keys, preferred_element_type=jnp.float32) * scale
    peak, total, rounded = softmax_state(scores, valid)
    mixed = jnp.einsum("sngl,lnd->sngd", rounded, values, preferred_element_type=jnp.float32)
    return (peak, total, mixed)


def combine(first, second):
    peak = jnp.maximum(first[0], second[0])
    left_scale = jnp.exp(first[0] - peak)
    right_scale = jnp.exp(second[0] - peak)
    total = first[1] * left_scale + second[1] * right_scale
    mixed = first[2] * left_scale[..., None] + second[2] * right_scale[..., None]
    return (peak, total, mixed)


def on_device(
    prompt_hidden,
    norm_gain,
    kv_weight,
    prompt_excess,
    prompt_owner,
    response_counts,
    queries,
    new_kv,
    response_cache,
    positions,
    out_weight,
):
    device = lax.axis_index("dev")
    rows = prompt_hidden.shape[0]
    width = prompt_hidden.shape[1]
    local_heads = kv_weight.shape[1]
    head_size = kv_weight.shape[3]
    slots = queries.shape[0]
    query_heads = queries.shape[1]
    group = query_heads // local_heads
    prompt_count = prompt_excess.shape[0]
    scale = head_size ** (-0.5)
    token_index = device * rows + jnp.arange(rows, dtype=jnp.int32)
    member, offsets, starts, lengths = prompt_layout(prompt_excess, token_index)
    hidden = prompt_hidden.astype(jnp.float32)
    normed = (
        hidden * lax.rsqrt(jnp.mean(hidden * hidden, axis=-1, keepdims=True) + 1e-05) * norm_gain
    ).astype(jnp.bfloat16)
    projected = jnp.dot(
        normed,
        kv_weight.reshape(width, local_heads * 2 * head_size),
        preferred_element_type=jnp.float32,
    )
    projected = projected.reshape(rows, local_heads, 2, head_size)
    prompt_keys = rotate(projected[:, :, 0], offsets).astype(jnp.bfloat16)
    prompt_values = projected[:, :, 1].astype(jnp.bfloat16)
    grouped = queries.reshape(slots, local_heads, group, head_size)
    slot_index = jnp.arange(slots, dtype=jnp.int32)
    chosen, present = slot_prompts(
        prompt_owner, response_counts, jnp.zeros((slots,), jnp.int32) + device, slot_index
    )
    cache_valid = jnp.arange(response_cache.shape[1], dtype=jnp.int32)[None, :] < positions[:, None]
    cache_state = state_each(
        grouped, response_cache[:, :, :, 0], response_cache[:, :, :, 1], cache_valid, scale
    )
    self_valid = jnp.ones((slots, 1), dtype=bool)
    self_state = state_each(
        grouped, new_kv[:, None, :, 0], new_kv[:, None, :, 1], self_valid, scale
    )
    first = first_slots(prompt_owner, response_counts)
    rank = jnp.clip(slot_index - first[chosen], 0, RESP - 1)
    entry = chosen * RESP + rank
    select = (
        (entry[None, :] == jnp.arange(prompt_count * RESP, dtype=jnp.int32)[:, None])
        & present[None, :]
    ).astype(jnp.float32)
    table = jnp.dot(
        select,
        queries.reshape(slots, query_heads * head_size).astype(jnp.float32),
        precision=lax.Precision.HIGHEST,
    )
    table = lax.psum(table, "dev").astype(jnp.bfloat16)
    table = table.reshape(prompt_count, RESP, local_heads, group, head_size)
    held = jnp.any(member, axis=0)
    first_prompt = jnp.sum((starts + lengths <= token_index[0]).astype(jnp.int32))
    reach = min(rows // PROMPT_MIN + 2, prompt_count)
    layout = (
        jnp.full((prompt_count, RESP, local_heads, group), -1e30, jnp.float32),
        jnp.zeros((prompt_count, RESP, local_heads, group), jnp.float32),
        jnp.zeros((prompt_count, RESP, local_heads, group, head_size), jnp.float32),
    )
    for step in range(reach):
        pick = jnp.minimum(first_prompt + step, prompt_count - 1)
        live = (first_prompt + step < prompt_count) & held[pick]
        reply_queries = lax.dynamic_index_in_dim(table, pick, 0, keepdims=False)
        reply_live = jnp.arange(RESP, dtype=jnp.int32) < response_counts[pick]
        row_member = (token_index >= starts[pick]) & (token_index < starts[pick] + lengths[pick])
        valid = live & reply_live[:, None] & row_member[None, :]
        fresh = state_shared(reply_queries, prompt_keys, prompt_values, valid, scale)
        earlier = tuple(
            (lax.dynamic_index_in_dim(part_now, pick, 0, keepdims=False) for part_now in layout)
        )
        merged = combine(earlier, fresh)
        layout = tuple(
            (
                lax.dynamic_update_index_in_dim(part_now, part_new, pick, 0)
                for part_now, part_new in zip(layout, merged)
            )
        )
    joined_peak, joined_total, joined_mixed = merged_2(layout, "dev", combine)
    flat_peak = joined_peak.reshape(prompt_count * RESP, local_heads, group)
    flat_total = joined_total.reshape(prompt_count * RESP, local_heads, group)
    flat_mixed = joined_mixed.reshape(prompt_count * RESP, local_heads, group, head_size)
    own_peak = jnp.take(flat_peak, entry, axis=0)
    own_total = jnp.take(flat_total, entry, axis=0)
    own_mixed = jnp.take(flat_mixed, entry, axis=0)
    prompt_state = (
        jnp.where(present[:, None, None], own_peak, -1e30),
        jnp.where(present[:, None, None], own_total, 0.0),
        jnp.where(present[:, None, None, None], own_mixed, 0.0),
    )
    final = combine(combine(prompt_state, cache_state), self_state)
    attended = (
        (final[2] / final[1][..., None]).reshape(slots, query_heads, head_size).astype(jnp.bfloat16)
    )
    flat = attended.reshape(slots, query_heads * head_size)
    weight_flat = out_weight.reshape(query_heads * head_size, out_weight.shape[2])
    head_terms = jnp.dot(
        lax.all_gather(flat, "dev", axis=0, tiled=True),
        weight_flat,
        preferred_element_type=jnp.float32,
    )
    block_out = lax.psum_scatter(head_terms, "role", scatter_dimension=0, tiled=True).astype(
        jnp.bfloat16
    )
    return (attended, block_out)


def solution(mesh):
    return jax.shard_map(
        on_device,
        mesh=mesh,
        in_specs=(
            P(("groups", "dev"), None),
            P(),
            P(None, "role", None, None),
            P("groups"),
            P("groups"),
            P("groups"),
            P(("groups", "dev"), "role", None),
            P(("groups", "dev"), "role", None, None),
            P(("groups", "dev"), None, "role", None, None),
            P(("groups", "dev")),
            P("role", None, "dev"),
        ),
        out_specs=(P(("groups", "dev"), "role", None), P(("groups", "role"), "dev")),
        check_vma=False,
    )
```

profile of v0, /device:TPU:1, one launch (start us, length us, event | category | flops | bytes accessed | tf_op | source)
XLA Modules:
  0.0 298.4 jit_solution(10407446676272909244)
XLA Ops:
  7.2 0.5 slice.31
  7.8 0.7 broadcast_add_fusion
  8.4 0.2 reduce-window.8
  8.6 1.9 bitcast_subtract_fusion.3
  11.8 0.7 broadcast_compare_fusion
  12.5 0.9 select_reduce_fusion.2
  13.4 1.3 fusion.107
  14.8 0.6 fusion.110
  16.3 0.7 fusion.109
  17.0 0.6 fusion.108
  17.6 0.7 add.228
  18.4 0.7 gather_fusion
  19.0 0.9 fusion.46
  19.9 64.6 %psum.7 = bf16[20,1024]{1,0:T(8,128)(2,1)S(1)} all-reduce(f32[20,1024]{1,0:T(8,128)S(1)} %fusion.46), channel_id=1, replica_groups=mesh['groups'=1,'role'=2,'dev'=16] {'dev'}, use_global_device_ids=true, to_apply=%region_9.10 | all-reduce | flops 20480 | bytes 122880 | tf_op jit(solution)/shard_map/psum | solution.py:158
  84.6 7.2 %reshape.412 = bf16[4096,512]{1,0:T(8,128)(2,1)} reshape(bf16[4096,2,2,128]{3,2,1,0:T(2,128)(2,1)} %param.17) | data formatting | bytes 8388608 | tf_op jit(solution)/shard_map/reshape | solution.py:127
  91.8 6.6 %copy.138 = bf16[512,4096]{1,0:T(8,128)(2,1)} copy(bf16[512,4096]{0,1:T(8,128)(2,1)} %bitcast.222) | data formatting | bytes 8388608 | tf_op jit(solution)/shard_map/dot_general | solution.py:125
  98.4 0.5 fusion.3
  99.0 3.6 %fusion.7 = f32[256,2,2,128]{0,3,2,1:T(8,128)S(1)} fusion(bf16[2,2,128,4096]{3,2,1,0:T(8,128)(2,1)} %bitcast.223, bf16[256,4096]{1,0:T(8,128)(2,1)S(1)} %copy-done.1, f32[4096]{0:T(1024)S(1)} %copy-done.7, f32[256]{0:T(256)S(1)} %add_rsqrt_fusion), kind=kOutput, calls=%fused_computation.18 | convolution fusion | flops 1077936128 | bytes 6833152 | tf_op jit(solution)/shard_map/dot_general | solution.py:125
  105.1 1.2 compare_and_fusion
  106.3 0.3 multiply_cosine_fusion
  107.2 0.6 compare_and_fusion.3
  107.9 0.2 fusion.112
  108.2 0.2 fusion.39
  108.3 0.2 fusion.30
  109.2 0.6 compare_and_fusion.1
  109.9 0.2 fusion.113
  110.2 0.2 fusion.27
  110.4 0.6 copy-done.2
  111.2 10.2 %fusion.106 = (bf16[16,256,2,1,128]{4,3,2,1,0:T(2,128)(2,1)}, bf16[16,256,2,1,128]{4,3,2,1,0:T(2,128)(2,1)}) fusion(bf16[16,256,2,2,128]{4,3,2,1,0:T(2,128)(2,1)} %param.23), kind=kLoop, calls=%fused_computation.189 | loop fusion | bytes 8388608 | tf_op jit(solution)/shard_map/slice | solution.py:140
  121.4 2.9 fusion.111
  124.5 0.1 fusion.59
  124.8 0.2 fusion.32
  125.1 0.2 fusion.41
  125.3 30.1 %all_gather.32 = f32[16,4,5,2,4]{2,4,3,1,0:T(4,128)S(1)} all-gather(f32[1,4,5,2,4]{2,4,3,1,0:T(4,128)S(1)} %get-tuple-element.219), channel_id=1, replica_groups=mesh['groups'=1,'role'=2,'dev'=16] {'dev'}, dimensions={0}, use_global_device_ids=true | all-gather | bytes 10880 | tf_op jit(solution)/shard_map/all_gather | solution.py:14
  155.4 33.3 %all_gather.29 = f32[16,4,5,2,4]{2,4,3,1,0:T(4,128)S(1)} all-gather(f32[1,4,5,2,4]{2,4,3,1,0:T(4,128)S(1)} %get-tuple-element.220), channel_id=1, replica_groups=mesh['groups'=1,'role'=2,'dev'=16] {'dev'}, dimensions={0}, use_global_device_ids=true | all-gather | bytes 10880 | tf_op jit(solution)/shard_map/all_gather | solution.py:14
  188.8 0.9 slice_bitcast_fusion.1
  189.7 22.4 %while.19 = (s32[]{:T(128)}, f32[4,5,2,4]{1,3,2,0:T(4,128)S(1)}, f32[4,5,2,4]{1,3,2,0:T(4,128)S(1)}, f32[4,5,2,4,128]{4,3,2,1,0:T(4,128)S(1)}, f32[16,4,5,2,4]{2...) while((s32[]{:T(128)}, f32[4,5,2,4]{1,3,2,0:T(4,128)S(1)}, ...), condition=%wide.region_15.16_spmd, body=%wide.region_14.15_spmd.sunk | while | flops 62405 | bytes 254871 | solution.py:19
  189.7 0.1 copy.236
  190.0 1.2 fusion.123
  191.2 0.1 copy.236
  191.5 1.2 fusion.123
  193.0 1.2 fusion.123
  194.5 1.2 fusion.123
  196.0 1.2 fusion.123
  197.5 1.2 fusion.123
  198.7 0.1 copy.236
  199.0 1.2 fusion.123
  200.2 0.1 copy.236
  200.5 1.2 fusion.123
  202.0 1.2 fusion.123
  203.5 1.2 fusion.123
  205.0 1.2 fusion.123
  206.5 1.2 fusion.123
  208.0 1.2 fusion.123
  209.5 1.2 fusion.123
  211.0 1.2 fusion.123
  212.3 0.6 gather_fusion.2
  213.1 0.6 gather_fusion.3
  214.4 0.6 gather_fusion.1
  215.0 2.7 fusion.24
  217.7 31.5 %all_gather.36 = bf16[256,1024]{1,0:T(8,128)(2,1)S(1)} all-gather(bf16[16,1024]{1,0:T(8,128)(2,1)S(1)} %convert_element_type.68), channel_id=1, replica_groups=mesh['groups'=1,'role'=2,'dev'=16] {'dev'}, dimensions={0}, use_global_device_ids=true | all-gather | bytes 557056 | tf_op jit(solution)/shard_map/all_gather | solution.py:205
  249.2 1.0 fusion.114
  250.2 39.8 %reduce-scatter.2.cloned.1.call-done = f32[128,256]{1,0:T(8,128)} async-done(((f32[256,256]{1,0:T(8,128)}), f32[128,256]{1,0:T(8,128)}) %reduce-scatter.2.cloned.1.call-update) | async-done | bytes 131088 | tf_op jit(solution)/shard_map/reduce_scatter | solution.py:209
  290.1 1.5 convert_element_type.69
  (116 shorter events, 6.6 us)
Async XLA Ops:
  7.2 242.0 %copy-start = (bf16[8,128,256]{2,1,0:T(8,128)(2,1)S(1)}, bf16[8,128,256]{2,1,0:T(8,128)(2,1)}, u32[]{:S(2)}) copy-start(bf16[8,128,256]{2,1,0:T(8,128)(2,1)} %param.25) | copy-start | bytes 1572868
  7.2 181.6 %all-gather.2.cloned.1.call-start = ((), (), s32[]{:S(2)}) async-start(), calls=%async_computation.1 | async-start | bytes 1392640 | tf_op jit(solution)/shard_map/all_gather | solution.py:14
  91.8 6.6 %copy-start.1 = (bf16[256,4096]{1,0:T(8,128)(2,1)S(1)}, bf16[256,4096]{1,0:T(8,128)(2,1)}, u32[]{:S(2)}) copy-start(bf16[256,4096]{1,0:T(8,128)(2,1)} %param.15) | copy-start | bytes 6291460
  91.8 7.1 %copy-start.7 = (f32[4096]{0:T(1024)S(1)}, f32[4096]{0:T(1024)}, u32[]{:S(2)}) copy-start(f32[4096]{0:T(1024)} %param.16) | copy-start | bytes 49156
  110.4 0.6 copy-start.2
  111.1 10.3 %copy-start.6 = (s32[16]{0:T(128)S(1)}, s32[16]{0:T(128)}, u32[]{:S(2)}) copy-start(s32[16]{0:T(128)} %param.24) | copy-start | bytes 196
  111.1 10.3 %copy-start.5 = (bf16[16,8,128]{2,1,0:T(8,128)(2,1)S(1)}, bf16[16,8,128]{2,1,0:T(8,128)(2,1)}, u32[]{:S(2)}) copy-start(bf16[16,8,128]{2,1,0:T(8,128)(2,1)} %param.21) | copy-start | bytes 98308
  111.1 13.4 %copy-start.3 = (bf16[16,2,2,128]{3,2,1,0:T(2,128)(2,1)S(1)}, bf16[16,2,2,128]{3,2,1,0:T(2,128)(2,1)}, u32[]{:S(2)}) copy-start(bf16[16,2,2,128]{3,2,1,0:T(2,128)(2,1)} %param.22) | copy-start | bytes 49156
  111.1 178.9 %reduce-scatter.2.cloned.1.call-start = ((), (), s32[]{:S(2)}) async-start(), calls=%async_computation.2 | async-start | bytes 393216 | tf_op jit(solution)/shard_map/reduce_scatter | solution.py:209
  217.7 73.9 %copy-start.4 = (bf16[16,2,4,128]{3,2,1,0:T(4,128)(2,1)}, bf16[16,2,4,128]{3,2,1,0:T(4,128)(2,1)S(1)}, u32[]{:S(2)}) copy-start(bf16[16,2,4,128]{3,2,1,0:T(4,128)(2,1)S(1)} %fusion.24) | copy-start | bytes 98308
Sparse Core Ops, SparseCore 0:
  111.2 66.7 all-gather.1
  250.3 39.6 reduce-scatter.1
where the time goes:
time: 300 us; the launch traced here: 298 us
  blocking collectives  160 us (53%)
  waiting for transfers between devices  39.9 us (13%)
  local copies, waits for them, and re-layouts  37.2 us (12%)
  other arithmetic  29.3 us (10%)
  between operations  20.1 us (7%)
  matrix products  12 us (4%)
    psum x1, blocking collectives, on_device(): table = lax.psum(table, 'dev').astype(jnp.bfloat16)  64.6 us
    all_gather x2, blocking collectives, merged_2(): gathered = jax.tree.map(lambda a: lax.all_gather(a, axis), part)  63.4 us
    reduce_scatter x1, waiting for transfers between devices, on_device(): lax.psum_scatter(head_terms, 'role', scatter_dimension=0, tiled=True)  39.8 us
    all_gather x1, blocking collectives, on_device(): lax.all_gather(flat, 'dev', axis=0, tiled=True)  31.5 us
    add x15, other arithmetic, combine(): first[2] * left_scale[..., None] + second[2] * right_scale[..., None]  17.5 us
    slice x1, local copies, waits for them, and re-layouts, on_device(): response_cache[:, :, :, 0]  10.2 us
    reshape x1, local copies, waits for them, and re-layouts, on_device(): kv_weight.reshape(width, local_heads * 2 * head_size)  7.22 us
    dot_general x1, local copies, waits for them, and re-layouts, on_device(): jnp.dot(normed, kv_weight.reshape(width, local_heads * 2 * head_size), pr...  6.6 us
  transfers between devices with their start and end apart: 2, of which 1 were waited for; matrix products, arithmetic and copies ran while one was open for 5% of the time, Pallas kernels for 0%

commit v1 on v0

v1 whole, which is shorter than its diff:
```python
import functools

import jax
import jax.numpy as jnp
from jax import lax
from jax.experimental import pallas as pl
from jax.experimental.pallas import tpu as pltpu
from jax.sharding import PartitionSpec as P

RESP = 5
PROMPT_MIN = 512
MESH = pl.DeviceIdType.MESH
LOW = -1e30
CHUNKS = 4

rope_base = 500000.0


def first_slots(owner, counts):
    order = jnp.arange(owner.shape[0], dtype=jnp.int32)
    earlier = (owner[:, None] == owner[None, :]) & (order[None, :] < order[:, None])
    return jnp.sum(jnp.where(earlier, counts[None, :], 0), axis=1)


def nt(a, b):
    return lax.dot_general(a, b, (((1,), (1,)), ((), ())), preferred_element_type=jnp.float32)


def nn(a, b):
    return jnp.dot(a, b, preferred_element_type=jnp.float32)


def kernel(
    cfg,
    hidden_hbm, gain_ref, kvw_hbm, q_ref, new_ref, cache_hbm, ow_hbm,
    cos_ref, sin_ref, target_ref, window_ref, row_code_ref, col_code_ref, pos_ref,
    attended_ref, block_ref,
    hidden, kvw, cache, ow, ow_far, normed, acc, keys, values, q_all,
    mix_all, stat_all, mix_mine, stat_mine, scores, cache_mix, att_rows, att_flat, att_all,
    local_sem, cache_sem, q_send, q_recv, mix_send, mix_recv, stat_send, stat_recv,
    att_send, att_recv, ow_send, ow_recv,
):
    n, roles, slots, heads, local_heads, context, head, used, padded = cfg
    group = heads // local_heads
    per = n // roles
    rows = slots * heads
    scale = head ** (-0.5)
    me = lax.axis_index("dev")
    role = lax.axis_index("role")
    width = hidden.shape[1]
    step = width // CHUNKS
    span = cache.shape[0] // CHUNKS

    hidden_copy = pltpu.make_async_copy(hidden_hbm, hidden, local_sem.at[CHUNKS])
    hidden_copy.start()
    kvw_copies = []
    for c in range(CHUNKS):
        part = pl.ds(c * step, step)
        kvw_copies.append(pltpu.make_async_copy(kvw_hbm.at[part], kvw.at[part], local_sem.at[c]))
        kvw_copies[-1].start()
    ow_copy = pltpu.make_async_copy(ow_hbm, ow, local_sem.at[CHUNKS + 1])
    ow_copy.start()
    cache_copies = []
    for c in range(CHUNKS):
        part = pl.ds(c * span, span)
        cache_copies.append(
            pltpu.make_async_copy(cache_hbm.at[part], cache.at[part], cache_sem.at[c])
        )
        cache_copies[-1].start()

    barrier = pltpu.get_barrier_semaphore()

    def greet(i, carry):
        other = lax.rem(me * roles + role + i, n * roles)
        pl.semaphore_signal(
            barrier,
            inc=1,
            device_id={"dev": other // roles, "role": lax.rem(other, roles)},
            device_id_type=MESH,
        )
        return carry

    lax.fori_loop(1, n * roles, greet, 0)
    pl.semaphore_wait(barrier, n * roles - 1)

    def q_copy(peer, slot):
        return pltpu.make_async_remote_copy(
            src_ref=q_ref, dst_ref=q_all.at[slot], send_sem=q_send.at[peer],
            recv_sem=q_recv.at[slot], device_id={"dev": peer}, device_id_type=MESH,
        )

    def mix_copy(peer, slot):
        return pltpu.make_async_remote_copy(
            src_ref=mix_mine, dst_ref=mix_all.at[slot, pl.ds(0, used)], send_sem=mix_send.at[peer],
            recv_sem=mix_recv.at[slot], device_id={"dev": peer}, device_id_type=MESH,
        )

    def stat_copy(peer, slot):
        return pltpu.make_async_remote_copy(
            src_ref=stat_mine, dst_ref=stat_all.at[slot], send_sem=stat_send.at[peer],
            recv_sem=stat_recv.at[slot], device_id={"dev": peer}, device_id_type=MESH,
        )

    def every(action):
        def body(o, carry):
            action(lax.rem(me + o, n))
            return carry

        lax.fori_loop(1, n, body, 0)

    every(lambda peer: q_copy(peer, me).start())
    q_all[me] = q_ref[...]

    def ow_far_copy(j):
        return pltpu.make_async_remote_copy(
            src_ref=ow_hbm, dst_ref=ow_far.at[j - 1], send_sem=ow_send.at[j - 1],
            recv_sem=ow_recv.at[j - 1],
            device_id={"role": lax.rem(role + roles - j, roles)}, device_id_type=MESH,
        )

    for j in range(1, roles):
        ow_far_copy(j).start()

    for e in range(n):
        mix_all[e, used:padded, :] = jnp.zeros((padded - used, head), jnp.bfloat16)

    hidden_copy.wait()
    block = 32

    def normalise(i, carry):
        part = pl.ds(pl.multiple_of(i * block, block), block)
        x = hidden[part, :].astype(jnp.float32)
        ratio = lax.rsqrt(jnp.mean(x * x, axis=-1, keepdims=True) + 1e-05)
        normed[part, :] = (x * ratio * gain_ref[...]).astype(jnp.bfloat16)
        return carry

    lax.fori_loop(0, hidden.shape[0] // block, normalise, 0)
    for c in range(CHUNKS):
        kvw_copies[c].wait()
        part = slice(c * step, (c + 1) * step)
        product = nn(normed[:, part], kvw[part, :])
        if c == 0:
            acc[...] = product
        else:
            acc[...] += product
    for k in range(local_heads):
        raw = acc[:, 2 * k * head : (2 * k + 1) * head]
        turned = jnp.concatenate([raw[:, head // 2 :], raw[:, : head // 2]], axis=1)
        keys[k] = (raw * cos_ref[...] + turned * sin_ref[...]).astype(jnp.bfloat16)
        values[k] = acc[:, (2 * k + 1) * head : (2 * k + 2) * head].astype(jnp.bfloat16)

    every(lambda peer: q_copy(peer, peer).wait_recv())
    target = target_ref[...]
    column = lax.broadcasted_iota(jnp.int32, (used, rows), 1)
    chosen = jnp.concatenate(
        [(target[:, :1] - e * rows == column).astype(jnp.float32) for e in range(n)], axis=1
    ).astype(jnp.bfloat16)
    table = nn(chosen, q_all[...].reshape(n * rows, head)).astype(jnp.bfloat16)
    share = used // local_heads
    peaks, totals, mixes = [], [], []
    for k in range(local_heads):
        mine = slice(k * share, (k + 1) * share)
        valid = target[mine, 1:2] == window_ref[0:1, :]
        s = jnp.where(valid, nt(table[mine], keys[k]) * scale, LOW)
        peak = jnp.max(s, axis=1, keepdims=True)
        w = jnp.where(valid, jnp.exp(s - peak), 0.0)
        peaks.append(peak)
        totals.append(jnp.sum(w, axis=1, keepdims=True))
        mixes.append(nn(w.astype(jnp.bfloat16), values[k]))
    mix_mine[...] = jnp.concatenate(mixes, axis=0).astype(jnp.bfloat16)
    lane = lax.broadcasted_iota(jnp.int32, (used, padded), 1)
    stats = jnp.where(
        lane == 0, jnp.concatenate(peaks, axis=0), jnp.where(lane == 1, jnp.concatenate(totals, axis=0), 0.0)
    )
    stats = jnp.concatenate([stats, jnp.zeros((padded - used, padded), jnp.float32)], axis=0)
    stat_mine[...] = stats.T[:8]

    def send_state(peer):
        stat_copy(peer, me).start()
        mix_copy(peer, me).start()

    every(send_state)
    mix_all[me, 0:used, :] = mix_mine[...]
    stat_all[me] = stat_mine[...]

    for c in range(CHUNKS):
        cache_copies[c].wait()
    line = 2 * local_heads * context

    def score(s, carry):
        part = pl.ds(pl.multiple_of(s * heads, heads), heads)
        block_rows = pl.ds(pl.multiple_of(s * line, line), line)
        scores[part, :] = nt(q_ref[part, :], cache[block_rows, :]) * scale
        return carry

    lax.fori_loop(0, slots, score, 0, unroll=4)
    col = lax.broadcasted_iota(jnp.int32, (rows, line), 1)
    row = lax.broadcasted_iota(jnp.int32, (rows, line), 0)
    own_head = lax.rem(row, heads) // group
    valid = (lax.rem(col, 2 * local_heads) == 2 * own_head) & (
        col // (2 * local_heads) < pos_ref[:, :1]
    )
    s = jnp.where(valid, scores[...], LOW)
    cache_peak = jnp.max(s, axis=1, keepdims=True)
    w = jnp.where(valid, jnp.exp(s - cache_peak), 0.0)
    cache_total = jnp.sum(w, axis=1, keepdims=True)
    scores[...] = pltpu.roll(w, 1, 1)

    def mix(s, carry):
        part = pl.ds(pl.multiple_of(s * heads, heads), heads)
        block_rows = pl.ds(pl.multiple_of(s * line, line), line)
        cache_mix[part, :] = nn(scores[part, :].astype(jnp.bfloat16), cache[block_rows, :])
        return carry

    lax.fori_loop(0, slots, mix, 0, unroll=4)

    fresh = new_ref[...]
    near = nt(q_ref[...], fresh) * scale
    fcol = lax.broadcasted_iota(jnp.int32, near.shape, 1)
    frow = lax.broadcasted_iota(jnp.int32, near.shape, 0)
    pair = 2 * (frow // group)
    self_score = jnp.max(jnp.where(fcol == pair, near, LOW), axis=1, keepdims=True)

    def wait_state(peer):
        stat_copy(peer, peer).wait_recv()
        mix_copy(peer, peer).wait_recv()

    every(wait_state)
    row_code = row_code_ref[:, :1]
    held = jnp.concatenate(
        [jnp.where(row_code == col_code_ref[e : e + 1, :], stat_all[e, 0:1, :], LOW) for e in range(n)],
        axis=1,
    )
    totals_all = jnp.concatenate([stat_all[e, 1:2, :] for e in range(n)], axis=1)
    peak = jnp.maximum(jnp.maximum(cache_peak, self_score), jnp.max(held, axis=1, keepdims=True))
    weight = jnp.where(held > 0.5 * LOW, jnp.exp(held - peak), 0.0)
    total = jnp.sum(weight * totals_all, axis=1, keepdims=True)
    mixed = nn(weight.astype(jnp.bfloat16), mix_all[...].reshape(n * padded, head))
    cache_weight = jnp.exp(cache_peak - peak)
    self_weight = jnp.exp(self_score - peak)
    total = total + cache_total * cache_weight + self_weight
    mixed = mixed + cache_mix[...] * cache_weight
    mixed = mixed + nn(jnp.where(fcol == pair + 1, self_weight, 0.0).astype(jnp.bfloat16), fresh)
    att = mixed / total
    att_rows[...] = att
    attended_ref[...] = att.astype(jnp.bfloat16)
    for h in range(heads):
        att_flat[:, h * head : (h + 1) * head] = att_rows[pl.ds(h, slots, stride=heads), :].astype(
            jnp.bfloat16
        )

    home = me // per
    place = lax.rem(me, per)

    def att_copy(peer, peer_role, from_role, slot):
        return pltpu.make_async_remote_copy(
            src_ref=att_flat, dst_ref=att_all.at[from_role, slot], send_sem=att_send.at[peer],
            recv_sem=att_recv.at[from_role, slot],
            device_id={"dev": peer, "role": peer_role}, device_id_type=MESH,
        )

    every(lambda peer: att_copy(peer, home, role, place).start())

    @pl.when(home != role)
    def _():
        att_copy(me, home, role, place).start()

    @pl.when(home == role)
    def _():
        att_all[role, place] = att_flat[...]

    for j in range(1, roles):
        ow_far_copy(j).wait()
    ow_copy.wait()

    def wait_att(i, carry):
        from_role = i // per
        slot = lax.rem(i, per)

        @pl.when(jnp.logical_not((from_role == role) & (role * per + slot == me)))
        def _():
            att_copy(me, role, from_role, slot).wait_recv()

        return carry

    lax.fori_loop(0, n, wait_att, 0)
    out = nn(att_all[role].reshape(per * slots, heads * head), ow[...])
    for j in range(1, roles):
        far = lax.rem(role + j, roles)
        out = out + nn(att_all[far].reshape(per * slots, heads * head), ow_far[j - 1])
    block_ref[...] = out.astype(jnp.bfloat16)

    every(lambda peer: q_copy(peer, me).wait_send())

    def sent_state(peer):
        stat_copy(peer, me).wait_send()
        mix_copy(peer, me).wait_send()

    every(sent_state)
    every(lambda peer: att_copy(peer, home, role, place).wait_send())

    @pl.when(home != role)
    def _():
        att_copy(me, home, role, place).wait_send()


def on_device(
    prompt_hidden,
    norm_gain,
    kv_weight,
    prompt_excess,
    prompt_owner,
    response_counts,
    queries,
    new_kv,
    response_cache,
    positions,
    out_weight,
):
    n = lax.axis_size("dev")
    roles = lax.axis_size("role")
    device = lax.axis_index("dev")
    rows, width = prompt_hidden.shape
    local_heads = kv_weight.shape[1]
    head = kv_weight.shape[3]
    slots, heads, _ = queries.shape
    group = heads // local_heads
    context = response_cache.shape[1]
    prompts = prompt_excess.shape[0]
    columns = out_weight.shape[2]
    reach = min(rows // PROMPT_MIN + 2, prompts)
    used = reach * RESP * heads
    padded = -(-used // 128) * 128
    i32 = jnp.int32

    lengths = PROMPT_MIN + prompt_excess
    upto = jnp.arange(prompts, dtype=i32)
    ends = jnp.sum(jnp.where(upto[None, :] <= upto[:, None], lengths[None, :], 0), axis=1)
    starts = ends - lengths
    tokens = device * rows + jnp.arange(rows, dtype=i32)
    prompt_id = jnp.sum((tokens[:, None] >= ends[None, :]).astype(i32), axis=1)
    member = prompt_id[:, None] == upto[None, :]
    offsets = tokens - jnp.sum(jnp.where(member, starts[None, :], 0), axis=1)
    lanes = jnp.arange(head, dtype=i32)
    half = head // 2
    freq = rope_base ** (-(lanes % half).astype(jnp.float32) * 2.0 / head)
    angles = offsets.astype(jnp.float32)[:, None] * freq[None, :]
    cosine = jnp.cos(angles)
    sine = jnp.where(lanes[None, :] < half, -1.0, 1.0) * jnp.sin(angles)

    all_first = jnp.sum((jnp.arange(n, dtype=i32)[:, None] * rows >= ends[None, :]).astype(i32), axis=1)
    first_prompt = jnp.sum((device * rows >= ends).astype(i32))
    window = jnp.broadcast_to((prompt_id - first_prompt)[None, :], (8, rows))

    first = first_slots(prompt_owner, response_counts)
    j = jnp.arange(padded, dtype=i32)
    share = reach * RESP * group
    k_of = j // share
    w_of = (j % share) // (RESP * group)
    r_of = (j % (RESP * group)) // group
    h_of = k_of * group + j % group
    inside = j < used
    p_of = first_prompt + w_of
    at = p_of[:used, None] == upto[None, :]
    seat = jnp.sum(jnp.where(at, (prompt_owner * slots + first)[None, :], 0), axis=1)
    count = jnp.sum(jnp.where(at, response_counts[None, :], 0), axis=1)
    live = r_of[:used] < count
    target = jnp.where(live, (seat + r_of[:used]) * heads + h_of[:used], -1)
    seen = jnp.where(live, w_of[:used], -1)
    target = jnp.where(jnp.arange(128, dtype=i32)[None, :] == 1, seen[:, None], target[:, None])

    col_code = ((all_first[:, None] + w_of[None, :]) * RESP + r_of[None, :]) * heads + h_of[None, :]
    col_code = jnp.where(inside[None, :], col_code, -2)

    rix = jnp.arange(slots * heads, dtype=i32)
    slot = rix // heads
    match = (
        (prompt_owner[None, :] == device)
        & (first[None, :] <= slot[:, None])
        & (slot[:, None] < (first + response_counts)[None, :])
    )
    entry = jnp.sum(
        jnp.where(match, upto[None, :] * RESP + slot[:, None] - first[None, :], 0), axis=1
    )
    row_code = jnp.where(jnp.any(match, axis=1), entry * heads + rix % heads, -1)
    row_code = jnp.broadcast_to(row_code[:, None], (slots * heads, 128))
    pos = jnp.broadcast_to(positions[:, None, None], (slots, heads, 128)).reshape(slots * heads, 128)

    line = 2 * local_heads * context
    bf16, f32 = jnp.bfloat16, jnp.float32
    dma = pltpu.SemaphoreType.DMA
    anywhere = pl.BlockSpec(memory_space=pl.ANY)
    vmem = pl.BlockSpec(memory_space=pltpu.VMEM)
    cfg = (n, roles, slots, heads, local_heads, context, head, used, padded)
    attended, block_out = pl.pallas_call(
        functools.partial(kernel, cfg),
        out_shape=(
            jax.ShapeDtypeStruct((slots * heads, head), bf16),
            jax.ShapeDtypeStruct((n // roles * slots, columns), bf16),
        ),
        in_specs=[anywhere, vmem, anywhere, vmem, vmem, anywhere, anywhere] + [vmem] * 7,
        out_specs=(vmem, vmem),
        scratch_shapes=[
            pltpu.VMEM((rows, width), bf16),
            pltpu.VMEM((width, local_heads * 2 * head), bf16),
            pltpu.VMEM((slots * line, head), bf16),
            pltpu.VMEM((heads * head, columns), bf16),
            pltpu.VMEM((roles - 1, heads * head, columns), bf16),
            pltpu.VMEM((rows, width), bf16),
            pltpu.VMEM((rows, local_heads * 2 * head), f32),
            pltpu.VMEM((local_heads, rows, head), bf16),
            pltpu.VMEM((local_heads, rows, head), bf16),
            pltpu.VMEM((n, slots * heads, head), bf16),
            pltpu.VMEM((n, padded, head), bf16),
            pltpu.VMEM((n, 8, padded), f32),
            pltpu.VMEM((used, head), bf16),
            pltpu.VMEM((8, padded), f32),
            pltpu.VMEM((slots * heads, line), f32),
            pltpu.VMEM((slots * heads, head), f32),
            pltpu.VMEM((slots * heads, head), f32),
            pltpu.VMEM((slots, heads * head), bf16),
            pltpu.VMEM((roles, n // roles, slots, heads * head), bf16),
            dma((CHUNKS + 2,)),
            dma((CHUNKS,)),
            dma((n,)),
            dma((n,)),
            dma((n,)),
            dma((n,)),
            dma((n,)),
            dma((n,)),
            dma((n,)),
            dma((roles, n // roles)),
            dma((roles - 1,)),
            dma((roles - 1,)),
        ],
        compiler_params=pltpu.CompilerParams(
            collective_id=0, has_side_effects=True, vmem_limit_bytes=56 * 1024 * 1024
        ),
    )(
        prompt_hidden,
        norm_gain.reshape(1, width),
        kv_weight.reshape(width, local_heads * 2 * head),
        queries.reshape(slots * heads, head),
        new_kv.reshape(slots * local_heads * 2, head),
        response_cache.reshape(slots * line, head),
        out_weight.reshape(heads * head, columns),
        cosine,
        sine,
        target,
        window,
        row_code,
        col_code,
        pos,
    )
    return (attended.reshape(slots, heads, head), block_out)


def solution(mesh):
    return jax.shard_map(
        on_device,
        mesh=mesh,
        in_specs=(
            P(("groups", "dev"), None),
            P(),
            P(None, "role", None, None),
            P("groups"),
            P("groups"),
            P("groups"),
            P(("groups", "dev"), "role", None),
            P(("groups", "dev"), "role", None, None),
            P(("groups", "dev"), None, "role", None, None),
            P(("groups", "dev")),
            P("role", None, "dev"),
        ),
        out_specs=(P(("groups", "dev"), "role", None), P(("groups", "role"), "dev")),
        check_vma=False,
    )
```

time: 300 us -> 68.8 us (0.23)
  the two profiles are of different devices: /device:TPU:1 before, /device:TPU:11 now
where the time goes in v1:
time: 68.8 us; the launch traced here: 68.3 us
  Pallas kernels  45.3 us (66%)
  local copies, waits for them, and re-layouts  12.9 us (19%)
  other arithmetic  9.44 us (14%)
  between operations  0.7 us (1%)
    pallas_call x1, Pallas kernels, on_device(): pl.pallas_call(functools.partial(kernel, cfg), out_shape=(jax.ShapeDtypeS...  45.3 us
    reshape x1, local copies, waits for them, and re-layouts, on_device(): kv_weight.reshape(width, local_heads * 2 * head)  7.21 us
    unnamed x2, local copies, waits for them, and re-layouts  2.85 us
    broadcast_in_dim x3, local copies, waits for them, and re-layouts, on_device(): jnp.broadcast_to(positions[:, None, None], (slots, heads, 128))  1.51 us

profile of v1, /device:TPU:11, one launch (start us, length us, event | category | flops | bytes accessed | tf_op | source)
XLA Modules:
  0.0 68.3 jit_solution(945769991242708136)
XLA Ops:
  0.6 0.7 broadcast_compare_fusion
  1.3 0.9 %select_reduce_fusion.3 = s32[4]{0:T(128)S(1)} fusion(s32[4]{0:T(128)} %param.16, s32[4]{0:T(128)} %param.15), kind=kLoop, calls=%fused_computation.11 | loop fusion | flops 76 | bytes 48 | tf_op jit(solution)/shard_map/reduce_sum | solution.py:22
  2.2 0.7 broadcast_add_fusion.1
  2.9 0.1 select_reduce_fusion.5
  3.0 0.1 convert_reduce_fusion.1
  3.1 0.1 convert_reduce_fusion
  3.2 1.3 %fusion.9 = (s32[]{:T(128)}, s32[4]{0:T(128)S(1)}) fusion(s32[4]{0:T(128)S(1)} %select_reduce_fusion.5, s32[]{:T(128)S(6)} %mul.83, s32[4]{0:T(128)} %param.14), kind=kLoop, calls=%fused_computation.47 | loop fusion | flops 19 | bytes 56 | tf_op jit(solution)/shard_map/reduce_sum | solution.py:352
  4.5 0.1 select_reduce_fusion
  4.6 0.6 broadcast_subtract_fusion
  5.2 0.7 broadcast_add_fusion
  6.0 0.7 fusion.12
  6.6 0.1 select_reduce_fusion.1
  6.8 0.7 %select_reduce_fusion.4 = (s32[80]{0:T(128)S(1)}, s32[80]{0:T(128)S(1)}) fusion(s32[4]{0:T(128)} %param.16, s32[80]{0:T(128)S(1)} %bitcast.13, s32[4]{0:T(128)S(1)} %get-tuple-element.15), kind=kLoop, calls=%fused_computation.13 | loop fusion | flops 1440 | bytes 992 | tf_op jit(solution)/shard_map/reduce_sum | solution.py:366
  7.5 0.7 add_select_fusion.col_code_ref
  8.2 0.6 broadcast_in_dim.177.window_ref
  8.8 0.7 %broadcast_in_dim.182 = s32[16,8]{1,0:T(8,128)S(1)} broadcast(s32[16]{0:T(128)} %param.20), dimensions={0} | broadcast | bytes 576 | tf_op jit(solution)/shard_map/broadcast_in_dim | solution.py:387
  9.5 0.1 broadcast_in_dim.183
  9.6 0.7 %broadcast_select_fusion.target_ref = s32[80,128]{1,0:T(8,128)} fusion(s32[80]{0:T(128)S(1)} %get-tuple-element.13, s32[80]{0:T(128)S(1)} %get-tuple-element.12, pred[128]{0:T(512)(128)(4,1)S(1)} %iota_compare_fusion.5), kind=kLoop, calls=%fused_computation.3 | loop fusion | flops 10240 | bytes 41728 | tf_op jit(solution)/shard_map/jit(_where)/select_n | solution.py:370
  10.3 0.7 %broadcast_in_dim.184.pos_ref = s32[128,128]{1,0:T(8,128)} broadcast(s32[128]{0:T(128)S(1)} %broadcast_in_dim.183), dimensions={0} | broadcast | bytes 66048 | tf_op jit(solution)/shard_map/broadcast_in_dim | solution.py:387
  11.0 0.7 %broadcast_in_dim.179.row_code_ref = s32[128,128]{1,0:T(8,128)} broadcast(s32[128]{0:T(128)S(1)} %fusion.3), dimensions={0} | broadcast | bytes 66048 | tf_op jit(solution)/shard_map/broadcast_in_dim | solution.py:386
  11.7 1.2 %fusion = (f32[256,128]{1,0:T(8,128)}, f32[256,128]{1,0:T(8,128)}) fusion(f32[128]{0:T(128)S(1)} %get-tuple-element.18, f32[128]{0:T(128)S(1)} %get-tuple-element.19, f32[256]{0:T(256)S(1)} %subtract_convert_fusion), kind=kLoop, calls=%fused_computation.2 | loop fusion | flops 65536 | bytes 264192 | tf_op jit(solution)/shard_map/mul | solution.py:349
  12.9 7.2 %reshape.189.kvw_hbm = bf16[4096,512]{1,0:T(8,128)(2,1)} reshape(bf16[4096,2,2,128]{3,2,1,0:T(2,128)(2,1)} %param.13) | data formatting | bytes 8388608 | tf_op jit(solution)/shard_map/reshape | solution.py:442
  20.2 45.3 %shard_map.122 = (bf16[128,128]{1,0:T(8,128)(2,1)}, bf16[128,256]{1,0:T(8,128)(2,1)}) custom-call(bf16[256,4096]{1,0:T(8,128)(2,1)} %hidden_hbm.1, f32[1,4096]{1,0:T(1,128)} %bitcast.11, bf16[4096,512]{1,0:T(8,128)(2,1)} %reshape.189.kvw_hbm, bf16[128,128]{1,0:T(8,128)(2,1)} %bitcast.9, bf16[64,128]{1,0:T(8,128)(2,1)} %bitcast.12, ...), custom_call_target="tpu_custom_call" | custom-call | tf_op jit(solution)/shard_map/pallas_call | solution.py:395
  65.5 1.4 %copy.15 = bf16[16,8,128]{2,1,0:T(8,128)(2,1)} copy(bf16[16,8,128]{2,1,0:T(8,128)(2,1)} %bitcast.10) | data formatting | bytes 65536
  66.8 1.5 %copy.16 = bf16[128,256]{1,0:T(8,128)(2,1)} copy(bf16[128,256]{1,0:T(8,128)(2,1)} %get-tuple-element.26) | data formatting | bytes 131072
  (12 shorter events, 0.1 us)

commit v2 on v1

v2 whole, which is shorter than its diff:
```python
import functools

import jax
import jax.numpy as jnp
from jax import lax
from jax.experimental import pallas as pl
from jax.experimental.pallas import tpu as pltpu
from jax.sharding import PartitionSpec as P

RESP = 5
PROMPT_MIN = 512
MESH = pl.DeviceIdType.MESH
LOW = -1e30
CHUNKS = 4

rope_base = 500000.0


def nt(a, b):
    return lax.dot_general(a, b, (((1,), (1,)), ((), ())), preferred_element_type=jnp.float32)


def nn(a, b):
    return jnp.dot(a, b, preferred_element_type=jnp.float32)


def kernel(
    cfg,
    hidden_hbm, gain_ref, kvw_hbm, q_ref, new_ref, cache_hbm, ow_hbm,
    freq_ref, excess_ref, owner_ref, count_ref, pos_ref,
    attended_ref, block_ref,
    hidden, kvx, wide, kvw, cos_ref, sin_ref, cache, ow, ow_far, normed, acc, keys, values, q_all,
    mix_all, stat_all, mix_mine, stat_mine, scores, cache_mix, att_rows, att_flat, att_all,
    local_sem, cache_sem, q_send, q_recv, mix_send, mix_recv, stat_send, stat_recv,
    att_send, att_pass, att_recv, ow_send, ow_recv,
):
    n, inner, roles, slots, heads, local_heads, context, head, reach, used, padded = cfg
    outer = n // inner
    group = heads // local_heads
    per = n // roles
    rows = slots * heads
    scale = head ** (-0.5)
    me = lax.axis_index("dev")
    role = lax.axis_index("role")
    width = hidden.shape[1]
    step = width // CHUNKS
    pairs = 2 * local_heads
    tokens = hidden.shape[0]
    prompts = excess_ref.shape[0]
    i32 = jnp.int32
    major, minor = me // inner, lax.rem(me, inner)
    span = cache.shape[0] // CHUNKS

    hidden_copy = pltpu.make_async_copy(hidden_hbm, hidden, local_sem.at[CHUNKS])
    hidden_copy.start()
    kvw_copies = []
    for c in range(CHUNKS):
        part = pl.ds(c * step * pairs, step * pairs)
        kvw_copies.append(pltpu.make_async_copy(kvw_hbm.at[part], kvx.at[part], local_sem.at[c]))
        kvw_copies[-1].start()
    ow_copy = pltpu.make_async_copy(ow_hbm, ow, local_sem.at[CHUNKS + 1])
    ow_copy.start()
    cache_copies = []
    for c in range(CHUNKS):
        part = pl.ds(c * span, span)
        cache_copies.append(
            pltpu.make_async_copy(cache_hbm.at[part], cache.at[part], cache_sem.at[c])
        )
        cache_copies[-1].start()

    barrier = pltpu.get_barrier_semaphore()

    def greet(i, carry):
        other = lax.rem(me * roles + role + i, n * roles)
        pl.semaphore_signal(
            barrier,
            inc=1,
            device_id={"dev": other // roles, "role": lax.rem(other, roles)},
            device_id_type=MESH,
        )
        return carry

    lax.fori_loop(1, n * roles, greet, 0)

    lengths = [PROMPT_MIN + excess_ref[p] for p in range(prompts)]
    ends = [lengths[0]]
    for p in range(1, prompts):
        ends.append(ends[-1] + lengths[p])
    owners = [owner_ref[p] for p in range(prompts)]
    counts = [count_ref[p] for p in range(prompts)]
    firsts = []
    for p in range(prompts):
        first = jnp.int32(0)
        for q in range(p):
            first = first + jnp.where(owners[q] == owners[p], counts[q], 0)
        firsts.append(first)

    def prompt_of(token):
        found = jnp.zeros_like(token)
        for p in range(prompts):
            found = found + jnp.where(token >= ends[p], 1, 0)
        return found

    def reply_of(index):
        k = jnp.zeros_like(index)
        for m in range(1, local_heads):
            k = k + jnp.where(index >= m * (used // local_heads), 1, 0)
        rest = index - k * (used // local_heads)
        w = jnp.zeros_like(index)
        for m in range(1, reach):
            w = w + jnp.where(rest >= m * RESP * group, 1, 0)
        rest = rest - w * (RESP * group)
        return w, lax.div(rest, group), k * group + lax.rem(rest, group)

    first_prompt = prompt_of(me * tokens)
    w_of, r_of, h_of = reply_of(lax.broadcasted_iota(i32, (used, 128), 0))
    seat = jnp.zeros_like(w_of)
    number = jnp.zeros_like(w_of)
    for p in range(prompts):
        here = first_prompt + w_of == p
        seat = jnp.where(here, owners[p] * slots + firsts[p], seat)
        number = jnp.where(here, counts[p], number)
    live = r_of < number
    target = jnp.where(live, (seat + r_of) * heads + h_of, -1)
    seen = jnp.where(live, w_of, -1)
    window = prompt_of(me * tokens + lax.broadcasted_iota(i32, (8, tokens), 1)) - first_prompt
    col_first = prompt_of(tokens * lax.broadcasted_iota(i32, (n, padded), 0))
    col_index = lax.broadcasted_iota(i32, (n, padded), 1)
    cw, cr, ch = reply_of(col_index)
    col_code = jnp.where(col_index < used, ((col_first + cw) * RESP + cr) * heads + ch, -2)
    row_index = lax.broadcasted_iota(i32, (rows, 128), 0)
    row_slot = lax.div(row_index, heads)
    row_code = jnp.full((rows, 128), -1, i32)
    for p in range(prompts):
        rank = row_slot - firsts[p]
        mine = (owners[p] == me) & (rank >= 0) & (rank < counts[p])
        row_code = jnp.where(mine, (p * RESP + rank) * heads + lax.rem(row_index, heads), row_code)

    half = head // 2
    token = me * tokens + lax.broadcasted_iota(i32, (tokens, head), 0)
    offset = token
    for p in range(prompts):
        offset = offset - jnp.where(token >= ends[p], lengths[p], 0)
    angle = offset.astype(jnp.float32) * freq_ref[...]
    cos_ref[...] = jnp.cos(angle)
    lane = lax.broadcasted_iota(i32, (tokens, head), 1)
    sine = jnp.sin(angle)
    sin_ref[...] = jnp.where(lane < half, -sine, sine)
    for e in range(n):
        mix_all[e, used:padded, :] = jnp.zeros((padded - used, head), jnp.bfloat16)

    pl.semaphore_wait(barrier, n * roles - 1)

    def peer_at(o, i):
        return lax.rem(major + o, outer) * inner + lax.rem(minor + i, inner)

    class Gather:
        def __init__(self, mine, everyone, send, recv):
            self.refs = mine, everyone, send, recv

        def copy(self, src, slot, o, i, peer):
            mine, everyone, send, recv = self.refs
            return pltpu.make_async_remote_copy(
                src_ref=src, dst_ref=everyone(slot), send_sem=send.at[o, i],
                recv_sem=recv.at[slot], device_id={"dev": peer}, device_id_type=MESH,
            )

        def own(self, o, i):
            return self.copy(self.refs[0], me, o, i, peer_at(o, i))

        def passed(self, o, i):
            slot = peer_at(o, 0)
            return self.copy(self.refs[1](slot), slot, o, i, peer_at(0, i))

        def start(self):
            for o in range(1, outer):
                self.own(o, 0).start()
            for i in range(1, inner):
                self.own(0, i).start()

        def forward(self):
            for o in range(1, outer):
                self.passed(o, 0).wait_recv()
                for i in range(1, inner):
                    self.passed(o, i).start()

        def finish(self):
            for o in range(outer):
                for i in range(1, inner):
                    slot = peer_at(o, i)
                    self.copy(self.refs[0], slot, 0, 0, me).wait_recv()

        def sent(self):
            for o in range(1, outer):
                self.own(o, 0).wait_send()
                for i in range(1, inner):
                    self.passed(o, i).wait_send()
            for i in range(1, inner):
                self.own(0, i).wait_send()

    q_net = Gather(q_ref, lambda e: q_all.at[e], q_send, q_recv)
    mix_net = Gather(mix_mine, lambda e: mix_all.at[e, pl.ds(0, used)], mix_send, mix_recv)
    stat_net = Gather(stat_mine, lambda e: stat_all.at[e], stat_send, stat_recv)
    q_net.start()
    q_all[me] = q_ref[...]

    def ow_far_copy(j):
        return pltpu.make_async_remote_copy(
            src_ref=ow_hbm, dst_ref=ow_far.at[j - 1], send_sem=ow_send.at[j - 1],
            recv_sem=ow_recv.at[j - 1],
            device_id={"role": lax.rem(role + roles - j, roles)}, device_id_type=MESH,
        )

    for j in range(1, roles):
        ow_far_copy(j).start()

    hidden_copy.wait()
    block = 32

    def normalise(i, carry):
        part = pl.ds(pl.multiple_of(i * block, block), block)
        x = hidden[part, :].astype(jnp.float32)
        ratio = lax.rsqrt(jnp.mean(x * x, axis=-1, keepdims=True) + 1e-05)
        normed[part, :] = (x * ratio * gain_ref[...]).astype(jnp.bfloat16)
        return carry

    lax.fori_loop(0, hidden.shape[0] // block, normalise, 0)
    tall = wide.shape[1]

    def unweave(i, carry):
        lot = lax.rem(i, 2)
        wide[lot] = kvx[pl.ds(pl.multiple_of(i * tall, tall), tall), :].astype(jnp.float32)
        part = pl.ds(pl.multiple_of(i * (tall // pairs), tall // pairs), tall // pairs)
        for m in range(pairs):
            kvw[part, m * head : (m + 1) * head] = wide[
                lot, pl.ds(m, tall // pairs, stride=pairs), :
            ].astype(jnp.bfloat16)
        return carry

    per_chunk = step * pairs // tall
    for c in range(CHUNKS):
        kvw_copies[c].wait()
        lax.fori_loop(c * per_chunk, (c + 1) * per_chunk, unweave, 0, unroll=2)
        if c == 0:
            q_net.forward()
        part = slice(c * step, (c + 1) * step)
        product = nn(normed[:, part], kvw[part, :])
        if c == 0:
            acc[...] = product
        else:
            acc[...] += product
    for k in range(local_heads):
        raw = acc[:, 2 * k * head : (2 * k + 1) * head]
        turned = jnp.concatenate([raw[:, head // 2 :], raw[:, : head // 2]], axis=1)
        keys[k] = (raw * cos_ref[...] + turned * sin_ref[...]).astype(jnp.bfloat16)
        values[k] = acc[:, (2 * k + 1) * head : (2 * k + 2) * head].astype(jnp.bfloat16)

    q_net.finish()
    column = lax.broadcasted_iota(jnp.int32, (used, rows), 1)
    chosen = jnp.concatenate(
        [(target[:, :1] - e * rows == column).astype(jnp.float32) for e in range(n)], axis=1
    ).astype(jnp.bfloat16)
    table = nn(chosen, q_all[...].reshape(n * rows, head)).astype(jnp.bfloat16)
    share = used // local_heads
    peaks, totals, mixes = [], [], []
    for k in range(local_heads):
        mine = slice(k * share, (k + 1) * share)
        valid = seen[mine, :1] == window[0:1, :]
        s = jnp.where(valid, nt(table[mine], keys[k]) * scale, LOW)
        peak = jnp.max(s, axis=1, keepdims=True)
        w = jnp.where(valid, jnp.exp(s - peak), 0.0)
        peaks.append(peak)
        totals.append(jnp.sum(w, axis=1, keepdims=True))
        mixes.append(nn(w.astype(jnp.bfloat16), values[k]))
    mix_mine[...] = jnp.concatenate(mixes, axis=0).astype(jnp.bfloat16)
    lane = lax.broadcasted_iota(jnp.int32, (used, padded), 1)
    stats = jnp.where(
        lane == 0, jnp.concatenate(peaks, axis=0), jnp.where(lane == 1, jnp.concatenate(totals, axis=0), 0.0)
    )
    stats = jnp.concatenate([stats, jnp.zeros((padded - used, padded), jnp.float32)], axis=0)
    stat_mine[...] = stats.T[:8]

    stat_net.start()
    mix_net.start()
    mix_all[me, 0:used, :] = mix_mine[...]
    stat_all[me] = stat_mine[...]

    for c in range(CHUNKS):
        cache_copies[c].wait()
    line = 2 * local_heads * context

    def score(s, carry):
        part = pl.ds(pl.multiple_of(s * heads, heads), heads)
        block_rows = pl.ds(pl.multiple_of(s * line, line), line)
        raw = nt(q_ref[part, :], cache[block_rows, :]) * scale
        held_here = lax.div(col, pairs) < pos_ref[s]
        scores[part, :] = jnp.where((lax.rem(col, pairs) == 2 * own_head) & held_here, raw, LOW)
        return carry

    col = lax.broadcasted_iota(i32, (heads, line), 1)
    own_head = lax.div(lax.broadcasted_iota(i32, (heads, line), 0), group)

    lax.fori_loop(0, slots, score, 0, unroll=4)
    stat_net.forward()
    mix_net.forward()
    s = scores[...]
    cache_peak = jnp.max(s, axis=1, keepdims=True)
    w = jnp.where(s > 0.5 * LOW, jnp.exp(s - cache_peak), 0.0)
    cache_total = jnp.sum(w, axis=1, keepdims=True)
    scores[...] = pltpu.roll(w, 1, 1)

    def mix(s, carry):
        part = pl.ds(pl.multiple_of(s * heads, heads), heads)
        block_rows = pl.ds(pl.multiple_of(s * line, line), line)
        cache_mix[part, :] = nn(scores[part, :].astype(jnp.bfloat16), cache[block_rows, :])
        return carry

    lax.fori_loop(0, slots, mix, 0, unroll=4)

    fresh = new_ref[...]
    near = nt(q_ref[...], fresh) * scale
    fcol = lax.broadcasted_iota(jnp.int32, near.shape, 1)
    frow = lax.broadcasted_iota(jnp.int32, near.shape, 0)
    pair = 2 * (frow // group)
    self_score = jnp.max(jnp.where(fcol == pair, near, LOW), axis=1, keepdims=True)

    stat_net.finish()
    mix_net.finish()
    row_code = row_code[:, :1]
    held = jnp.concatenate(
        [jnp.where(row_code == col_code[e : e + 1, :], stat_all[e, 0:1, :], LOW) for e in range(n)],
        axis=1,
    )
    totals_all = jnp.concatenate([stat_all[e, 1:2, :] for e in range(n)], axis=1)
    peak = jnp.maximum(jnp.maximum(cache_peak, self_score), jnp.max(held, axis=1, keepdims=True))
    weight = jnp.where(held > 0.5 * LOW, jnp.exp(held - peak), 0.0)
    total = jnp.sum(weight * totals_all, axis=1, keepdims=True)
    mixed = nn(weight.astype(jnp.bfloat16), mix_all[...].reshape(n * padded, head))
    cache_weight = jnp.exp(cache_peak - peak)
    self_weight = jnp.exp(self_score - peak)
    total = total + cache_total * cache_weight + self_weight
    mixed = mixed + cache_mix[...] * cache_weight
    mixed = mixed + nn(jnp.where(fcol == pair + 1, self_weight, 0.0).astype(jnp.bfloat16), fresh)
    att = mixed / total
    att_rows[...] = att
    attended_ref[...] = att.astype(jnp.bfloat16)
    for h in range(heads):
        att_flat[:, h * head : (h + 1) * head] = att_rows[pl.ds(h, slots, stride=heads), :].astype(
            jnp.bfloat16
        )

    home = me // per
    place = lax.rem(me, per)

    fold = outer // roles

    def att_copy(src, from_role, o, slot, sem, peer, peer_role):
        return pltpu.make_async_remote_copy(
            src_ref=src, dst_ref=att_all.at[from_role, slot], send_sem=sem,
            recv_sem=att_recv.at[from_role, slot],
            device_id={"dev": peer, "role": peer_role}, device_id_type=MESH,
        )

    def att_own(o, i):
        return att_copy(att_flat, role, o, place, att_send.at[o, i], peer_at(o, i), home)

    def att_passed(from_role, o, i):
        slot = o * inner + minor
        return att_copy(
            att_all.at[from_role, slot], from_role, o, slot,
            att_pass.at[from_role, o, i], peer_at(0, i), role,
        )

    for o in range(1, outer):
        att_own(o, 0).start()
    for i in range(1, inner):
        att_own(0, i).start()

    @pl.when(home != role)
    def _():
        att_own(0, 0).start()

    @pl.when(home == role)
    def _():
        att_all[role, place] = att_flat[...]

    for j in range(1, roles):
        ow_far_copy(j).wait()
    ow_copy.wait()

    for o in range(fold):
        for from_role in range(roles):

            @pl.when(role * fold + o != major)
            def _():
                att_passed(from_role, o, 0).wait_recv()
                for i in range(1, inner):
                    att_passed(from_role, o, i).start()

            @pl.when((role * fold + o == major) & (from_role != role))
            def _():
                att_passed(from_role, o, 0).wait_recv()

    for o in range(fold):
        for from_role in range(roles):
            for i in range(1, inner):
                slot = o * inner + lax.rem(minor + i, inner)
                att_copy(att_flat, from_role, o, slot, att_send.at[0, 0], me, role).wait_recv()

    out = nn(att_all[role].reshape(per * slots, heads * head), ow[...])
    for j in range(1, roles):
        far = lax.rem(role + j, roles)
        out = out + nn(att_all[far].reshape(per * slots, heads * head), ow_far[j - 1])
    block_ref[...] = out.astype(jnp.bfloat16)

    q_net.sent()
    stat_net.sent()
    mix_net.sent()
    for o in range(1, outer):
        att_own(o, 0).wait_send()
    for i in range(1, inner):
        att_own(0, i).wait_send()

    @pl.when(home != role)
    def _():
        att_own(0, 0).wait_send()

    for o in range(fold):

        @pl.when(role * fold + o != major)
        def _():
            for from_role in range(roles):
                for i in range(1, inner):
                    att_passed(from_role, o, i).wait_send()


def on_device(
    prompt_hidden,
    norm_gain,
    kv_weight,
    prompt_excess,
    prompt_owner,
    response_counts,
    queries,
    new_kv,
    response_cache,
    positions,
    out_weight,
):
    n = lax.axis_size("dev")
    roles = lax.axis_size("role")
    rows, width = prompt_hidden.shape
    local_heads = kv_weight.shape[1]
    head = kv_weight.shape[3]
    slots, heads, _ = queries.shape
    group = heads // local_heads
    context = response_cache.shape[1]
    prompts = prompt_excess.shape[0]
    columns = out_weight.shape[2]
    reach = min(rows // PROMPT_MIN + 2, prompts)
    used = reach * RESP * heads
    padded = -(-used // 128) * 128
    inner = 1
    while inner * inner < n:
        inner *= 2
    half = head // 2
    freq = rope_base ** (-jnp.arange(half, dtype=jnp.float32) * 2.0 / head)
    freq = jnp.concatenate([freq, freq])[None, :]
    line = 2 * local_heads * context
    bf16, f32 = jnp.bfloat16, jnp.float32
    dma = pltpu.SemaphoreType.DMA
    anywhere = pl.BlockSpec(memory_space=pl.ANY)
    vmem = pl.BlockSpec(memory_space=pltpu.VMEM)
    smem = pl.BlockSpec(memory_space=pltpu.SMEM)
    cfg = (n, inner, roles, slots, heads, local_heads, context, head, reach, used, padded)
    attended, block_out = pl.pallas_call(
        functools.partial(kernel, cfg),
        out_shape=(
            jax.ShapeDtypeStruct((slots * heads, head), bf16),
            jax.ShapeDtypeStruct((n // roles * slots, columns), bf16),
        ),
        in_specs=[anywhere, vmem, anywhere, vmem, vmem, anywhere, anywhere] + [vmem] + [smem] * 4,
        out_specs=(vmem, vmem),
        scratch_shapes=[
            pltpu.VMEM((rows, width), bf16),
            pltpu.VMEM((width * local_heads * 2, head), bf16),
            pltpu.VMEM((2, 128 * local_heads * 2, head), f32),
            pltpu.VMEM((width, local_heads * 2 * head), bf16),
            pltpu.VMEM((rows, head), f32),
            pltpu.VMEM((rows, head), f32),
            pltpu.VMEM((slots * line, head), bf16),
            pltpu.VMEM((heads * head, columns), bf16),
            pltpu.VMEM((roles - 1, heads * head, columns), bf16),
            pltpu.VMEM((rows, width), bf16),
            pltpu.VMEM((rows, local_heads * 2 * head), f32),
            pltpu.VMEM((local_heads, rows, head), bf16),
            pltpu.VMEM((local_heads, rows, head), bf16),
            pltpu.VMEM((n, slots * heads, head), bf16),
            pltpu.VMEM((n, padded, head), bf16),
            pltpu.VMEM((n, 8, padded), f32),
            pltpu.VMEM((used, head), bf16),
            pltpu.VMEM((8, padded), f32),
            pltpu.VMEM((slots * heads, line), f32),
            pltpu.VMEM((slots * heads, head), f32),
            pltpu.VMEM((slots * heads, head), f32),
            pltpu.VMEM((slots, heads * head), bf16),
            pltpu.VMEM((roles, n // roles, slots, heads * head), bf16),
            dma((CHUNKS + 2,)),
            dma((CHUNKS,)),
            dma((n // inner, inner)),
            dma((n,)),
            dma((n // inner, inner)),
            dma((n,)),
            dma((n // inner, inner)),
            dma((n,)),
            dma((n // inner, inner)),
            dma((roles, n // inner // roles, inner)),
            dma((roles, n // roles)),
            dma((roles - 1,)),
            dma((roles - 1,)),
        ],
        compiler_params=pltpu.CompilerParams(
            collective_id=0, has_side_effects=True, vmem_limit_bytes=56 * 1024 * 1024
        ),
    )(
        prompt_hidden,
        norm_gain.reshape(1, width),
        kv_weight.reshape(width * local_heads * 2, head),
        queries.reshape(slots * heads, head),
        new_kv.reshape(slots * local_heads * 2, head),
        response_cache.reshape(slots * line, head),
        out_weight.reshape(heads * head, columns),
        freq,
        prompt_excess,
        prompt_owner,
        response_counts,
        positions,
    )
    return (attended.reshape(slots, heads, head), block_out)


def solution(mesh):
    return jax.shard_map(
        on_device,
        mesh=mesh,
        in_specs=(
            P(("groups", "dev"), None),
            P(),
            P(None, "role", None, None),
            P("groups"),
            P("groups"),
            P("groups"),
            P(("groups", "dev"), "role", None),
            P(("groups", "dev"), "role", None, None),
            P(("groups", "dev"), None, "role", None, None),
            P(("groups", "dev")),
            P("role", None, "dev"),
        ),
        out_specs=(P(("groups", "dev"), "role", None), P(("groups", "role"), "dev")),
        check_vma=False,
    )
```

time: 68.8 us -> 43.5 us (0.63)
  the two profiles are of different devices: /device:TPU:11 before, /device:TPU:1 now
where the time goes in v2:
time: 43.5 us; the launch traced here: 43.2 us
  Pallas kernels  39.1 us (90%)
  local copies, waits for them, and re-layouts  2.85 us (7%)
  between operations  0.64 us (1%)
  other arithmetic  0.6 us (1%)
    pallas_call x1, Pallas kernels, on_device(): pl.pallas_call(functools.partial(kernel, cfg), out_shape=(jax.ShapeDtypeS...  39.1 us
    unnamed x2, local copies, waits for them, and re-layouts  2.85 us

profile of v2, /device:TPU:1, one launch (start us, length us, event | category | flops | bytes accessed | tf_op | source)
XLA Modules:
  0.0 43.2 jit_solution(13685224039872985532)
XLA Ops:
  0.6 0.6 %maximum_bitcast_fusion.freq_ref = f32[1,128]{1,0:T(1,128)} fusion(f32[64]{0:T(128)S(1)} %multiply_power_fusion), kind=kLoop, calls=%fused_computation | loop fusion | flops 128 | bytes 768 | tf_op jit(solution)/shard_map/broadcast_in_dim | solution.py:468
  1.2 39.1 %shard_map.122 = (bf16[128,128]{1,0:T(8,128)(2,1)}, bf16[128,256]{1,0:T(8,128)(2,1)}) custom-call(bf16[256,4096]{1,0:T(8,128)(2,1)} %hidden_hbm.1, f32[1,4096]{1,0:T(1,128)} %bitcast.14, bf16[16384,128]{1,0:T(8,128)(2,1)} %bitcast.9, bf16[128,128]{1,0:T(8,128)(2,1)} %bitcast.12, bf16[64,128]{1,0:T(8,128)(2,1)} %bitcast.15, bf16[16384,128]{1,0:T(8,128)(2,1)} %bitcast.10, ...), custom_call_target="tpu_custom_call" | custom-call | tf_op jit(solution)/shard_map/pallas_call | solution.py:476
  40.4 1.4 %copy.15 = bf16[16,8,128]{2,1,0:T(8,128)(2,1)} copy(bf16[16,8,128]{2,1,0:T(8,128)(2,1)} %bitcast.13) | data formatting | bytes 65536
  41.7 1.5 %copy.16 = bf16[128,256]{1,0:T(8,128)(2,1)} copy(bf16[128,256]{1,0:T(8,128)(2,1)} %get-tuple-element.9) | data formatting | bytes 131072
  (1 shorter events, 0.0 us)

commit v3 on v2

--- a/solution.py
+++ b/solution.py
@@ -2,6 +2,7 @@
 
 import jax
 import jax.numpy as jnp
+import numpy as np
 from jax import lax
 from jax.experimental import pallas as pl
 from jax.experimental.pallas import tpu as pltpu
@@ -224,25 +225,27 @@
         normed[part, :] = (x * ratio * gain_ref[...]).astype(jnp.bfloat16)
         return carry
 
-    lax.fori_loop(0, hidden.shape[0] // block, normalise, 0)
+    lax.fori_loop(0, hidden.shape[0] // block, normalise, 0, unroll=2)
+    q_net.forward()
     tall = wide.shape[1]
 
     def unweave(i, carry):
-        lot = lax.rem(i, 2)
-        wide[lot] = kvx[pl.ds(pl.multiple_of(i * tall, tall), tall), :].astype(jnp.float32)
-        part = pl.ds(pl.multiple_of(i * (tall // pairs), tall // pairs), tall // pairs)
-        for m in range(pairs):
-            kvw[part, m * head : (m + 1) * head] = wide[
-                lot, pl.ds(m, tall // pairs, stride=pairs), :
-            ].astype(jnp.bfloat16)
+        short = tall // pairs
+        for lot in range(2):
+            at = 2 * i + lot
+            wide[lot] = kvx[pl.ds(pl.multiple_of(at * tall, tall), tall), :].astype(jnp.float32)
+        for lot in range(2):
+            part = pl.ds(pl.multiple_of((2 * i + lot) * short, short), short)
+            for m in range(pairs):
+                kvw[part, m * head : (m + 1) * head] = wide[
+                    lot, pl.ds(m, short, stride=pairs), :
+                ].astype(jnp.bfloat16)
         return carry
 
-    per_chunk = step * pairs // tall
+    per_chunk = step * pairs // (2 * tall)
     for c in range(CHUNKS):
         kvw_copies[c].wait()
-        lax.fori_loop(c * per_chunk, (c + 1) * per_chunk, unweave, 0, unroll=2)
-        if c == 0:
-            q_net.forward()
+        lax.fori_loop(c * per_chunk, (c + 1) * per_chunk, unweave, 0)
         part = slice(c * step, (c + 1) * step)
         product = nn(normed[:, part], kvw[part, :])
         if c == 0:
@@ -432,6 +435,11 @@
             for from_role in range(roles):
                 for i in range(1, inner):
                     att_passed(from_role, o, i).wait_send()
+
+
+def settle(attended_ref, block_ref, attended_out, block_out):
+    attended_out[...] = attended_ref[...]
+    block_out[...] = block_ref[...]
 
 
 def on_device(
@@ -464,8 +472,8 @@
     while inner * inner < n:
         inner *= 2
     half = head // 2
-    freq = rope_base ** (-jnp.arange(half, dtype=jnp.float32) * 2.0 / head)
-    freq = jnp.concatenate([freq, freq])[None, :]
+    freq = np.float32(rope_base) ** (-np.arange(half, dtype=np.float32) * np.float32(2.0 / head))
+    freq = jnp.asarray(np.concatenate([freq, freq])[None, :].astype(np.float32))
     line = 2 * local_heads * context
     bf16, f32 = jnp.bfloat16, jnp.float32
     dma = pltpu.SemaphoreType.DMA
@@ -536,6 +544,15 @@
         response_counts,
         positions,
     )
+    attended, block_out = pl.pallas_call(
+        settle,
+        out_shape=(
+            jax.ShapeDtypeStruct(attended.shape, bf16),
+            jax.ShapeDtypeStruct(block_out.shape, bf16),
+        ),
+        in_specs=[vmem, vmem],
+        out_specs=(vmem, vmem),
+    )(attended, block_out)
     return (attended.reshape(slots, heads, head), block_out)
 
 

time: 43.5 us -> 41.5 us (0.954)
  local copies, waits for them, and re-layouts: 2.85 us -> 0 us
  Pallas kernels: 39.1 us -> 40.6 us
  other arithmetic: 0.6 us -> 0 us
    unnamed x2 -> x0, local copies, waits for them, and re-layouts: 2.85 us -> none
    pallas_call x0 -> x1, Pallas kernels: none -> 1.5 us  [on_device(): pl.pallas_call(settle, out_shape=(jax.ShapeDtypeStruct(attended.shape, bf...]
    broadcast_in_dim x1 -> x0, other arithmetic: 0.59 us -> none  [on_device(): freq = jnp.concatenate([freq, freq])[None, :]]
where the time goes in v3:
time: 41.5 us; the launch traced here: 41.3 us
  Pallas kernels  40.6 us (98%)
  between operations  0.64 us (2%)
    pallas_call x1, Pallas kernels, on_device(): pl.pallas_call(functools.partial(kernel, cfg), out_shape=(jax.ShapeDtypeS...  39.1 us
    pallas_call x1, Pallas kernels, on_device(): pl.pallas_call(settle, out_shape=(jax.ShapeDtypeStruct(attended.shape, bf...  1.5 us

profile of v3, /device:TPU:1, one launch (start us, length us, event | category | flops | bytes accessed | tf_op | source)
XLA Modules:
  0.0 41.3 jit_solution(1075893394302181200)
XLA Ops:
  0.6 39.1 %shard_map.131 = (bf16[128,128]{1,0:T(8,128)(2,1)}, bf16[128,256]{1,0:T(8,128)(2,1)}) custom-call(bf16[256,4096]{1,0:T(8,128)(2,1)} %hidden_hbm.1, f32[1,4096]{1,0:T(1,128)} %bitcast.11, bf16[16384,128]{1,0:T(8,128)(2,1)} %bitcast.7, bf16[128,128]{1,0:T(8,128)(2,1)} %bitcast.10, bf16[64,128]{1,0:T(8,128)(2,1)} %bitcast.12, bf16[16384,128]{1,0:T(8,128)(2,1)} %bitcast.8, ...), custom_call_target="tpu_custom_call" | custom-call | tf_op jit(solution)/shard_map/pallas_call | solution.py:484
  39.8 1.5 %shard_map.132 = (bf16[128,128]{1,0:T(8,128)(2,1)}, bf16[128,256]{1,0:T(8,128)(2,1)}) custom-call(bf16[128,128]{1,0:T(8,128)(2,1)} %get-tuple-element.6.attended_ref, bf16[128,256]{1,0:T(8,128)(2,1)} %get-tuple-element.7.block_ref), custom_call_target="tpu_custom_call" | custom-call | tf_op jit(solution)/shard_map/pallas_call | solution.py:547
